TPU v7x, 32 devices: a whole 2x2x4 slice. The times are simulated.
32 devices in a mesh: grp: 4 (over z), dp: 8 (over y, x, core).
Axes of the slice: x: 2, y: 2, z: 4, core: 2. Of those that a mesh axis runs over, the one named last changes fastest.
Arguments:
- tokens: bfloat16 [4096, 3584], P(('grp', 'dp')), may hold values from -120 to 120, as said below
- lengths: int32 [32, 4], P(('grp', 'dp')), may hold values from 0 to 128, as said below
- dest: int32 [32, 4], P(('grp', 'dp')), may hold values from -1 to 3, as said below
- gain: float32 [3584], replicated, may hold values from 0.5 to 1.5
- weight: bfloat16 [3584, 10240], P('dp', 'grp'), may hold values from -0.09375 to 0.09375
Outputs:
- projected: bfloat16 [2048, 10240], P('dp', 'grp')
Inputs may be any that keep to these rules, and one draw needn't show every extreme that they name: The tokens of one row have a common scale, and so have those of one feature. A device's live rows are the sum of its lengths; rows after them are padding. Within the devices sharing a dp index, live rows fill ceil(live rows / 32) blocks on each device and 8 blocks in all. dest is -1 exactly for a device's blocks past its live rows and an owner along grp otherwise. Within the devices sharing a dp index, every owner receives exactly 2 blocks and no device sends more than 1 block to one owner.
All inputs are finite; a program needn't handle non-finite values.
Results may differ from a plain program's by a relative error of at most 0.0049.
Values may be sent and summed in bfloat16 or wider, within the bound.
A program may use at most 64 MiB of HBM per device.

v0:
```python
import jax
import jax.numpy as jnp
from jax import lax
from jax.sharding import PartitionSpec as P

BLK = 32
OWN_BLK = 2


EPS = 1e-06


def group_layout(dest_all, own_blocks):
    groups, slots_in = dest_all.shape
    flat_dest = dest_all.reshape(-1)
    flat_index = jnp.arange(groups * slots_in, dtype=jnp.int32)
    earlier = flat_index[None, :] < flat_index[:, None]
    same_dest = flat_dest[:, None] == flat_dest[None, :]
    source = flat_index // slots_in
    owner_rank = jnp.sum((same_dest & earlier).astype(jnp.int32), axis=1)
    pair_rank = jnp.sum(
        (same_dest & earlier & (source[:, None] == source[None, :])).astype(jnp.int32), axis=1
    )
    matches = (flat_dest[:, None, None] == jnp.arange(groups, dtype=jnp.int32)[None, :, None]) & (
        owner_rank[:, None, None] == jnp.arange(own_blocks, dtype=jnp.int32)[None, None, :]
    )
    picked = jnp.sum(jnp.where(matches, flat_index[:, None, None], 0), axis=0)
    return (picked, pair_rank)


def block_keys(blocks, lens_all, slots_in):
    doc_ends = jnp.cumsum(lens_all, axis=1)
    source = blocks // slots_in
    within = blocks % slots_in
    offset = jnp.arange(BLK, dtype=jnp.int32)
    position = (within[:, None] * BLK + offset[None, :]).reshape(-1)
    row_source = jnp.broadcast_to(source[:, None], (blocks.shape[0], BLK)).reshape(-1)
    row_ends = doc_ends[row_source]
    doc_index = jnp.sum((position[:, None] >= row_ends).astype(jnp.int32), axis=1)
    is_live = position < row_ends[:, -1]
    doc_keys = row_source * lens_all.shape[1] + doc_index
    slots = lens_all.shape[0] * lens_all.shape[1]
    onehot = (doc_keys[:, None] == jnp.arange(slots, dtype=jnp.int32)[None, :]) & is_live[:, None]
    return onehot


def doc_squares(rows, onehot):
    widened = rows.astype(jnp.float32)
    square = jnp.sum(widened * widened, axis=1)
    return jnp.sum(jnp.where(onehot, square[:, None], 0.0), axis=0)


def apply_scale(rows, onehot, totals, lens_flat, gain):
    features = rows.shape[1]
    mean_square = totals / (jnp.maximum(lens_flat, 1).astype(jnp.float32) * features)
    inverse = lax.rsqrt(mean_square + EPS)
    scale = jnp.sum(jnp.where(onehot, inverse[None, :], 0.0), axis=1)
    return (rows.astype(jnp.float32) * scale[:, None] * gain[None, :]).astype(jnp.bfloat16)


def fold_rows(rows_all, weight):
    return jnp.dot(
        rows_all,
        lax.all_gather(weight, "dp", axis=0, tiled=True),
        preferred_element_type=jnp.float32,
    ).astype(jnp.bfloat16)


def per_device(tokens, lengths, dest, gain, weight):
    groups = lax.axis_size("grp")
    slots_in = 2 * OWN_BLK
    features = tokens.shape[1]
    pair_most = max(1, (slots_in + groups - 1) // groups)
    lens_all, dest_all = (
        lax.all_gather(lengths, "grp", axis=0, tiled=True),
        lax.all_gather(dest, "grp", axis=0, tiled=True),
    )
    lens_flat = lens_all.reshape(-1)
    picked, pair_rank = group_layout(dest_all, OWN_BLK)
    my_index = lax.axis_index("grp")
    my_blocks = lax.dynamic_index_in_dim(picked, my_index, 0, keepdims=False)
    my_dest = dest[0]
    local_index = jnp.arange(slots_in, dtype=jnp.int32)
    my_pair = jnp.sum(
        (
            (my_dest[:, None] == my_dest[None, :]) & (local_index[None, :] < local_index[:, None])
        ).astype(jnp.int32),
        axis=1,
    )
    slot_ids = jnp.arange(groups * pair_most, dtype=jnp.int32)
    send_pick = (my_dest[None, :] == (slot_ids // pair_most)[:, None]) & (
        my_pair[None, :] == (slot_ids % pair_most)[:, None]
    )
    parcel = jnp.dot(
        send_pick.astype(jnp.bfloat16),
        tokens.reshape(slots_in, BLK * features),
        preferred_element_type=jnp.float32,
    ).astype(jnp.bfloat16)
    arrived = lax.all_to_all(parcel, "grp", split_axis=0, concat_axis=0, tiled=True)
    take_slot = my_blocks // slots_in * pair_most + pair_rank[my_blocks]
    take_onehot = (take_slot[:, None] == slot_ids[None, :]).astype(jnp.bfloat16)
    owned_rows = jnp.dot(take_onehot, arrived, preferred_element_type=jnp.float32).astype(
        jnp.bfloat16
    )
    owned_rows = owned_rows.reshape(OWN_BLK * BLK, features)
    raw_all = lax.all_gather(owned_rows, "grp", axis=0, tiled=True)
    group_onehot = block_keys(picked.reshape(-1), lens_all, slots_in)
    group_totals = doc_squares(raw_all, group_onehot)
    rows_all = apply_scale(raw_all, group_onehot, group_totals, lens_flat, gain)
    return fold_rows(rows_all, weight)


def solution(mesh):
    placed = (
        P(("grp", "dp"), None),
        P(("grp", "dp"), None),
        P(("grp", "dp"), None),
        P(),
        P("dp", "grp"),
    )
    return jax.shard_map(
        per_device, mesh=mesh, in_specs=placed, out_specs=P("dp", "grp"), check_vma=False
    )
```

profile of v0, /device:TPU:0, one launch (start us, length us, event | category | flops | bytes accessed | tf_op | source)
XLA Modules:
  0.0 209.6 jit_solution(7032493428231819487)
XLA Ops:
  6.5 0.9 convert_reduce_fusion.3
  7.5 1.9 reshape.291
  9.3 1.3 fusion
  10.6 0.5 broadcast.368
  11.1 1.9 reduce.9
  13.0 0.0 copy-start
  13.0 1.9 reshape.328
  14.9 6.3 %all-to-all-start = ((bf16[4,2,57344]{2,1,0:T(2,128)(2,1)}), bf16[4,2,57344]{2,1,0:T(2,128)(2,1)S(1)}, u32[]{:S(2)}, u32[]{:S(2)}) async-start(bf16[4,2,57344]{2,1,0:T(2,128)(2,1)} %reshape.328), calls=%async_computation | async-start | bytes 1835008 | tf_op jit(solution)/shard_map/all_to_all | solution.py:99
  21.2 0.0 all-gather.5.cloned.1.call-start
  21.2 0.0 copy-done
  21.2 20.8 %all-gather = s32[4,1,4]{2,1,0:T(1,128)S(1)} all-gather(s32[1,1,4]{2,1,0:T(1,128)S(1)} %bitcast.21), channel_id=1, replica_groups=mesh['grp'=4,'dp'=8] {'grp'}, dimensions={0}, use_global_device_ids=true | all-gather | bytes 80 | tf_op jit(solution)/shard_map/all_gather | solution.py:76
  42.0 0.6 broadcast.366
  42.6 0.7 reduce.8
  43.3 0.1 eq.134
  43.4 0.2 convert_reduce_fusion.2
  43.6 0.1 select_reduce_fusion.2
  43.8 0.2 dynamic-slice_reduce_fusion
  44.0 0.6 gather_fusion
  44.7 0.0 all-to-all-done
  44.7 0.9 reshape.329
  45.5 1.3 convolution_convert_fusion.1
  46.8 0.0 copy-start.1
  46.8 1.2 reshape.292
  48.0 0.0 all-gather.5.cloned.1.call-update
  48.1 0.0 all-gather.7.cloned.1.call-start
  48.1 0.7 all-gather.7.cloned.1.call-update
  48.8 0.0 copy-start.2
  48.8 13.2 %all-gather.1 = s32[4,1,4]{2,1,0:T(1,128)S(1)} all-gather(s32[1,1,4]{2,1,0:T(1,128)S(1)} %bitcast.22), channel_id=1, replica_groups=mesh['grp'=4,'dp'=8] {'grp'}, dimensions={0}, use_global_device_ids=true | all-gather | bytes 80 | tf_op jit(solution)/shard_map/all_gather | solution.py:75
  62.1 0.1 copy.15
  62.2 0.1 reshape.293
  62.3 0.1 iota_add_fusion
  62.3 0.1 add.116
  62.4 0.1 add.121
  62.6 0.2 reduce_window_sum.11
  62.7 0.1 mul.53
  62.8 0.1 broadcast_in_dim.32
  62.9 0.1 mul.49
  63.0 0.1 broadcast_in_dim.33
  63.0 0.1 reshape.294
  63.1 0.7 gather_fusion.1
  63.9 0.2 convert_reduce_fusion
  64.1 0.2 fusion.9
  64.3 28.6 %all-gather.5.cloned.1.call-done = bf16[256,3584]{1,0:T(8,128)(2,1)} async-done(((bf16[64,3584]{1,0:T(8,128)(2,1)}), bf16[256,3584]{1,0:T(8,128)(2,1)}) %all-gather.5.cloned.1.call-update) | async-done | bytes 1835024 | tf_op jit(solution)/shard_map/all_gather | solution.py:106
  92.9 1.9 fusion.1
  94.8 0.1 select_reduce_fusion.1
  94.9 0.1 select_reduce_fusion
  95.0 94.9 %all-gather.7.cloned.1.call-done = bf16[3584,2560]{1,0:T(8,128)(2,1)} async-done(((bf16[448,2560]{1,0:T(8,128)(2,1)}), bf16[3584,2560]{1,0:T(8,128)(2,1)}) %all-gather.7.cloned.1.call-update) | async-done | bytes 18350096 | tf_op jit(solution)/shard_map/all_gather | solution.py:64
  190.0 12.8 %convolution_convert_fusion.2 = bf16[256,2560]{1,0:T(8,128)(2,1)} fusion(bf16[3584,2560]{1,0:T(8,128)(2,1)} %all-gather.7.cloned.1.call-done, bf16[256,3584]{1,0:T(8,128)(2,1)} %all-gather.5.cloned.1.call-done, f32[3584]{0:T(1024)S(1)} %copy-done.2, f32[256]{0:T(256)S(1)} %select_reduce_fusion), kind=kOutput, calls=%fused_computation.7 | convolution fusion | flops 4701945856 | bytes 21511168 | tf_op jit(solution)/shard_map/dot_general | solution.py:62
  (15 shorter events, 0.1 us)
Async XLA Ops:
  13.0 8.2 %copy-start = (s32[1,4]{1,0:T(1,128)S(1)}, s32[1,4]{1,0:T(1,128)}, u32[]{:S(2)}) copy-start(s32[1,4]{1,0:T(1,128)} %param.7) | copy-start | bytes 52
  14.9 29.8 %all-to-all-start = ((bf16[4,2,57344]{2,1,0:T(2,128)(2,1)}), bf16[4,2,57344]{2,1,0:T(2,128)(2,1)S(1)}, u32[]{:S(2)}, u32[]{:S(2)}) async-start(bf16[4,2,57344]{2,1,0:T(2,128)(2,1)} %reshape.328), calls=%async_computation | async-start | bytes 1835008 | tf_op jit(solution)/shard_map/all_to_all | solution.py:99
  21.2 71.7 %all-gather.5.cloned.1.call-start = ((), (), s32[]{:S(2)}) async-start(), calls=%async_computation.1 | async-start | bytes 2293760 | tf_op jit(solution)/shard_map/all_gather | solution.py:106
  46.8 2.0 copy-start.1
  48.1 141.9 %all-gather.7.cloned.1.call-start = ((), (), s32[]{:S(2)}) async-start(), calls=%async_computation.2 | async-start | bytes 20643840 | tf_op jit(solution)/shard_map/all_gather | solution.py:64
  48.8 141.2 %copy-start.2 = (f32[3584]{0:T(1024)S(1)}, f32[3584]{0:T(1024)}, u32[]{:S(2)}) copy-start(f32[3584]{0:T(1024)} %param.8) | copy-start | bytes 43012
Sparse Core Ops, SparseCore 0:
  48.2 44.6 all-gather.4
  94.8 95.1 all-gather.6
where the time goes:
time: 210 us
  waiting for transfers between devices  124 us (59%)
  blocking collectives  34.1 us (16%)
  matrix products  15.4 us (7%)
  between operations  13.5 us (6%)
  local copies, waits for them, and re-layouts  9.32 us (4%)
  other arithmetic  6.66 us (3%)
  starting transfers between devices  6.39 us (3%)
    all_gather x1, waiting for transfers between devices, fold_rows(): lax.all_gather(weight, 'dp', axis=0, tiled=True)  94.9 us
    all_gather x1, waiting for transfers between devices, per_device(): raw_all = lax.all_gather(owned_rows, 'grp', axis=0, tiled=True)  28.6 us
    all_gather x1, blocking collectives, per_device(): lax.all_gather(dest, 'grp', axis=0, tiled=True)  20.8 us
    all_gather x1, blocking collectives, per_device(): lax.all_gather(lengths, 'grp', axis=0, tiled=True)  13.2 us
    dot_general x1, matrix products, fold_rows(): jnp.dot(rows_all, lax.all_gather(weight, 'dp', axis=0, tiled=True), prefe...  12.8 us
    all_to_all x1, starting transfers between devices, per_device(): lax.all_to_all(parcel, 'grp', split_axis=0, concat_axis=0, tiled=True)  6.35 us
  transfers between devices with their start and end apart: 3, of which 2 were waited for; matrix products, arithmetic and copies ran while one was open for 3% of the time, Pallas kernels for 0%

commit v1 on v0

v1 whole, which is shorter than its diff:
```python
import functools
import math

import jax
import jax.numpy as jnp
from jax import lax
from jax.experimental import pallas as pl
from jax.experimental.pallas import tpu as pltpu
from jax.sharding import PartitionSpec as P

BLK = 32
OWN_BLK = 2
EPS = 1e-06
MESH = pl.DeviceIdType.MESH


def kernel(cfg, lens_ref, dest_ref, tok_ref, gain_ref, w_ref, out_ref,
           wbuf, tbuf, gbuf, dbuf, abuf, acc, load_sem, ws, wr, zs, zr, ds_, dr):
    groups, side, pieces, features, split = cfg
    chips = side * side
    rows = w_ref.shape[0]
    cols = w_ref.shape[1]
    part = rows // pieces
    wide = 2 * rows
    mine = tbuf.shape[1]
    docs = lens_ref.shape[1]
    grp = lax.axis_index("grp")
    dp = lax.axis_index("dp")
    core = dp % 2
    lo = (dp // 2) % side
    hi = dp // (2 * side)

    def shard(c, dl, dh):
        return 2 * (((hi + dh) % side) * side + (lo + dl) % side) + c

    def first(c, j):
        return shard(c, j * (1 - c), j * c)

    def second(c, j):
        return shard(c, j * c, j * (1 - c))

    def corner(c, j, k):
        return shard(c, j * (1 - c) + k * c, j * c + k * (1 - c))

    sib = dp + 1 - 2 * core
    steps = range(1, side)
    edge = []
    for j in steps:
        edge.append((len(edge), "a", j, 0))
    for j in steps:
        edge.append((len(edge), "b", j, 0))
    diag = []
    for j in steps:
        for k in steps:
            diag.append((len(edge) + len(diag), "c", j, k))
    flows = len(edge) + len(diag)

    def origin(c, kind, j, k):
        if kind == "a":
            return first(c, side - j)
        if kind == "b":
            return second(c, side - j)
        return corner(c, side - j, side - k)

    def view(slot, q):
        return wbuf.at[pl.ds(pl.multiple_of(slot * rows + q * part, 16), part)]

    def wcopy(slot, q, idx, target):
        return pltpu.make_async_remote_copy(
            src_ref=view(slot, q), dst_ref=view(slot, q),
            send_sem=ws.at[idx, q], recv_sem=wr.at[idx, q],
            device_id={"dp": target}, device_id_type=MESH)

    def zview(src):
        return gbuf.at[src]

    def zcopies(way, s, src, target):
        return (
            pltpu.make_async_remote_copy(
                src_ref=zview(src), dst_ref=zview(src),
                send_sem=zs.at[way, s - 1], recv_sem=zr.at[way, s - 1],
                device_id={"grp": target}, device_id_type=MESH),
            pltpu.make_async_remote_copy(
                src_ref=dbuf.at[src], dst_ref=dbuf.at[src],
                send_sem=ds_.at[way, s - 1], recv_sem=dr.at[way, s - 1],
                device_id={"grp": target}, device_id_type=MESH),
        )

    load = pltpu.make_async_copy(
        w_ref, wbuf.at[pl.ds(pl.multiple_of(dp * rows, 16), rows)], load_sem.at[0])
    load.start()
    dload = pltpu.make_async_copy(dest_ref, dbuf.at[grp], load_sem.at[1])
    dload.start()

    barrier = pltpu.get_barrier_semaphore()
    for j in steps:
        pl.semaphore_signal(barrier, inc=1, device_id={"dp": first(core, j)}, device_id_type=MESH)
        pl.semaphore_signal(barrier, inc=1, device_id={"dp": second(core, j)}, device_id_type=MESH)
    pl.semaphore_signal(barrier, inc=1, device_id={"dp": sib}, device_id_type=MESH)

    @pl.when(grp > 0)
    def _():
        pl.semaphore_signal(barrier, inc=1, device_id={"grp": grp - 1}, device_id_type=MESH)

    @pl.when(grp < groups - 1)
    def _():
        pl.semaphore_signal(barrier, inc=1, device_id={"grp": grp + 1}, device_id_type=MESH)

    load.wait()
    ends = (grp + groups - 1) // groups + (2 * groups - 2 - grp) // groups
    pl.semaphore_wait(barrier, 2 * (side - 1) + 1 + ends)

    sent = []

    def go(copy):
        copy.start()
        sent.append(copy)

    for q in range(pieces):
        for n, kind, j, k in edge:
            go(wcopy(dp, q, n, first(core, j) if kind == "a" else second(core, j)))
        go(wcopy(dp, q, flows, sib))

    position = lax.broadcasted_iota(jnp.int32, (mine, 1), 0)
    square = jnp.zeros((mine, 1), jnp.float32)
    for h in range(chips):
        x = (tok_ref[h] if split else tok_ref[:, h * wide:(h + 1) * wide]).astype(jnp.float32)
        square = square + jnp.sum(x * x, axis=1, keepdims=True)
    scale = jnp.zeros((mine, 1), jnp.float32)
    end = jnp.int32(0)
    for c in range(docs):
        length = lens_ref[0, c]
        mask = (position >= end) & (position < end + length)
        total = jnp.sum(jnp.where(mask, square, 0.0), axis=0, keepdims=True)
        count = jnp.full((1, 1), jnp.maximum(length, 1), jnp.int32).astype(jnp.float32) * features
        scale = scale + jnp.where(mask, lax.rsqrt(total / count + EPS), 0.0)
        end = end + length
    for h in range(chips):
        x = (tok_ref[h] if split else tok_ref[:, h * wide:(h + 1) * wide]).astype(jnp.float32)
        g = gain_ref[h] if split else gain_ref[:, h * wide:(h + 1) * wide]
        tbuf[h] = (x * scale * g[0:1]).astype(jnp.bfloat16)
    tload = pltpu.make_async_copy(tbuf, zview(grp), load_sem.at[0])
    tload.start()
    dload.wait()
    tload.wait()

    def zsend(s):
        right = (grp - (s - 1) >= 0) & (grp < groups - 1)
        left = (grp + (s - 1) <= groups - 1) & (grp > 0)

        @pl.when(right)
        def _():
            for copy in zcopies(0, s, (grp - (s - 1) + groups) % groups, grp + 1):
                copy.start()

        @pl.when(left)
        def _():
            for copy in zcopies(1, s, (grp + (s - 1)) % groups, grp - 1):
                copy.start()

    def zrecv(s):
        @pl.when(grp - s >= 0)
        def _():
            for copy in zcopies(0, s, (grp - s + groups) % groups, grp):
                copy.wait_recv()

        @pl.when(grp + s <= groups - 1)
        def _():
            for copy in zcopies(1, s, (grp + s) % groups, grp):
                copy.wait_recv()

        if s < groups - 1:
            zsend(s + 1)

    def zdone(s):
        @pl.when((grp - (s - 1) >= 0) & (grp < groups - 1))
        def _():
            for copy in zcopies(0, s, (grp - (s - 1) + groups) % groups, grp):
                copy.wait_send()

        @pl.when((grp + (s - 1) <= groups - 1) & (grp > 0))
        def _():
            for copy in zcopies(1, s, (grp + (s - 1)) % groups, grp):
                copy.wait_send()

    zsend(1)

    def wrecv(entry, q):
        n, kind, j, k = entry
        slot = origin(core, kind, j, k)
        wcopy(slot, q, n, sib).wait_recv()
        if kind == "a":
            for far in steps:
                idx = len(edge) + (j - 1) * (side - 1) + far - 1
                go(wcopy(slot, q, idx, second(core, far)))
        go(wcopy(slot, q, flows + 1 + n, sib))

    def srecv(entry, q):
        if entry is None:
            wcopy(sib, q, flows, sib).wait_recv()
        else:
            n, kind, j, k = entry
            wcopy(origin(1 - core, kind, j, k), q, flows + 1 + n, sib).wait_recv()

    events = []
    for q in range(pieces):
        events.append((2.0 * (q + 1) / pieces, 0, functools.partial(
            lambda q: [wrecv(e, q) for e in edge], q)))
    for s in range(1, groups):
        events.append((0.8 * s, 1, functools.partial(zrecv, s)))
    events.sort(key=lambda e: e[:2])
    for _, _, act in events:
        act()

    out_rows = out_ref.shape[0]
    lane = lax.broadcasted_iota(jnp.int32, (8, mine), 1)
    slots_in = mine // BLK
    dests = [dbuf[g] for g in range(groups)]
    turned = [[d] + [pltpu.roll(d, BLK * t, 1) for t in range(1, slots_in)] for d in dests]
    row = lax.broadcasted_iota(jnp.int32, (out_rows, mine), 0)
    col = lax.broadcasted_iota(jnp.int32, (out_rows, mine), 1)
    same = (row % BLK) == (col % BLK)
    picks = []
    for g in range(groups):
        rank = jnp.zeros((8, mine), jnp.int32)
        for t in range(1, slots_in):
            rank = rank + jnp.where((turned[g][t] == dests[g]) & (lane >= BLK * t), 1, 0)
        for e in range(g):
            for t in range(slots_in):
                rank = rank + jnp.where(turned[e][t] == dests[g], 1, 0)
        place = jnp.where(dests[g] >= 0, dests[g] * OWN_BLK + rank, -1)
        hit = same & (place[0:1] == row // BLK)
        picks.append(jnp.where(hit, 1.0, 0.0).astype(jnp.bfloat16))
    pick = jnp.concatenate(picks, axis=1)

    @pl.loop(0, chips)
    def _(h):
        blocks = jnp.concatenate([gbuf[g, h] for g in range(groups)], axis=0)
        abuf[h] = jnp.dot(pick, blocks, preferred_element_type=jnp.float32).astype(jnp.bfloat16)

    tile = math.gcd(cols, 512)

    def chip_dot(chip, where):
        return jnp.dot(
            abuf[chip], wbuf[pl.ds(pl.multiple_of(chip * wide, 16), wide), where],
            preferred_element_type=jnp.float32)

    for q in range(pieces):
        for e in [None] + edge:
            srecv(e, q)

    near = [(0, 0)] + [(j, 0) for j in steps] + [(0, j) for j in steps]

    @pl.loop(0, cols // tile)
    def _(i):
        where = pl.ds(pl.multiple_of(i * tile, tile), tile)
        total = None
        for dl, dh in near:
            term = chip_dot(shard(0, dl, dh) // 2, where)
            total = term if total is None else total + term
        acc[:, where] = total

    for q in range(pieces):
        for e in diag:
            wrecv(e, q)
    for q in range(pieces):
        for e in diag:
            srecv(e, q)

    @pl.loop(0, cols // tile)
    def _(i):
        where = pl.ds(pl.multiple_of(i * tile, tile), tile)
        total = acc[:, where]
        for dl in steps:
            for dh in steps:
                total = total + chip_dot(shard(0, dl, dh) // 2, where)
        out_ref[:, where] = total.astype(out_ref.dtype)

    for copy in sent:
        copy.wait_send()
    for s in range(1, groups):
        zdone(s)


def per_device(sizes, tokens, lengths, dest, gain, weight):
    groups, n_dp = sizes
    chips = n_dp // 2
    side = math.isqrt(chips)
    assert side * side * 2 == n_dp
    mine, features = tokens.shape
    rows, cols = weight.shape
    wide = 2 * rows
    split = wide % 128 != 0
    pieces = 4 if rows % 64 == 0 else 1
    flows = side * side - 1
    if split:
        tokens = tokens.reshape(mine, chips, wide).transpose(1, 0, 2)
        gain = jnp.broadcast_to(gain.reshape(chips, 1, wide), (chips, 8, wide))
    else:
        gain = jnp.broadcast_to(gain.reshape(1, features), (8, features))
    dest_rows = jnp.broadcast_to(jnp.repeat(dest[0], BLK)[None, :], (8, mine))
    out_rows = groups * OWN_BLK * BLK
    vmem = pl.BlockSpec(memory_space=pltpu.VMEM)
    dma = pltpu.SemaphoreType.DMA
    return pl.pallas_call(
        functools.partial(kernel, (groups, side, pieces, features, split)),
        out_shape=jax.ShapeDtypeStruct((out_rows, cols), jnp.bfloat16),
        in_specs=[
            pl.BlockSpec(memory_space=pltpu.SMEM), vmem, vmem, vmem,
            pl.BlockSpec(memory_space=pl.ANY),
        ],
        out_specs=vmem,
        scratch_shapes=[
            pltpu.VMEM((n_dp * rows, cols), jnp.bfloat16),
            pltpu.VMEM((chips, mine, wide), jnp.bfloat16),
            pltpu.VMEM((groups, chips, mine, wide), jnp.bfloat16),
            pltpu.VMEM((groups, 8, mine), jnp.int32),
            pltpu.VMEM((chips, out_rows, wide), jnp.bfloat16),
            pltpu.VMEM((out_rows, cols), jnp.float32),
            dma((2,)),
            dma((2 * flows + 1, pieces)),
            dma((2 * flows + 1, pieces)),
            dma((2, groups - 1)),
            dma((2, groups - 1)),
            dma((2, groups - 1)),
            dma((2, groups - 1)),
        ],
        compiler_params=pltpu.CompilerParams(
            collective_id=0, has_side_effects=True, vmem_limit_bytes=62 * 2**20),
    )(lengths, dest_rows, tokens, gain, weight)


def solution(mesh):
    placed = (
        P(("grp", "dp"), None),
        P(("grp", "dp"), None),
        P(("grp", "dp"), None),
        P(),
        P("dp", "grp"),
    )
    sizes = (mesh.shape["grp"], mesh.shape["dp"])
    return jax.shard_map(
        functools.partial(per_device, sizes), mesh=mesh, in_specs=placed,
        out_specs=P("dp", "grp"), check_vma=False
    )
```

time: 210 us -> 91.4 us (0.44)
  waiting for transfers between devices: 124 us -> 0 us
  Pallas kernels: 0 us -> 85.9 us
  blocking collectives: 34.1 us -> 0 us
  matrix products: 15.4 us -> 0 us
  between operations: 13.5 us -> 0.01 us
  other arithmetic: 6.66 us -> 0 us
  starting transfers between devices: 6.39 us -> 0 us
  local copies, waits for them, and re-layouts: 9.32 us -> 5.23 us
    all_gather x2 -> x0, waiting for transfers between devices: 124 us -> none  [the longest x1 94.9 us: fold_rows(): lax.all_gather(weight, 'dp', axis=0, tiled=True)]
    pallas_call x0 -> x1, Pallas kernels: none -> 85.9 us  [per_device(): pl.pallas_call(functools.partial(kernel, (groups, side, pieces, features,...]
    all_gather x2 -> x0, blocking collectives: 34.1 us -> none  [the longest x1 20.8 us: per_device(): lax.all_gather(dest, 'grp', axis=0, tiled=True)]
    dot_general x3 -> x0, matrix products: 15.4 us -> none  [the longest x1 12.8 us: fold_rows(): jnp.dot(rows_all, lax.all_gather(weight, 'dp', axis=0, tiled=True), prefe...]
    all_to_all x1 -> x0, starting transfers between devices: 6.35 us -> none  [per_device(): lax.all_to_all(parcel, 'grp', split_axis=0, concat_axis=0, tiled=True)]
    reduce_sum x7 -> x0, other arithmetic: 3.57 us -> none  [the longest x1 1.94 us: doc_squares(): square = jnp.sum(widened * widened, axis=1)]
    reshape x4 -> x0, local copies, waits for them, and re-layouts: 3.23 us -> none  [the longest x1 1.88 us: per_device(): tokens.reshape(slots_in, BLK * features)]
    broadcast_in_dim x2 -> x4, local copies, waits for them, and re-layouts: 0.14 us -> 2.77 us  [the longest x3 1.4 us: per_device(): dest_rows = jnp.broadcast_to(jnp.repeat(dest[0], BLK)[None, :], (8, mine))]
  transfers between devices with their start and end apart: 3 -> 0, of which waited for: 2 -> 0; matrix products, arithmetic and copies ran while one was open for 3% -> 0% of each run, Pallas kernels for 0% -> 0%
where the time goes in v1:
time: 91.4 us; the launch traced here: 91.1 us
  Pallas kernels  85.9 us (94%)
  local copies, waits for them, and re-layouts  5.23 us (6%)
    pallas_call x1, Pallas kernels, per_device(): pl.pallas_call(functools.partial(kernel, (groups, side, pieces, features,...  85.9 us
    unnamed x1, local copies, waits for them, and re-layouts  2.46 us

profile of v1, /device:TPU:0, one launch (start us, length us, event | category | flops | bytes accessed | tf_op | source)
XLA Modules:
  0.0 91.1 jit_solution(17503141520297034119)
XLA Ops:
  0.0 0.7 broadcast_in_dim.15
  0.7 0.1 broadcast_in_dim.16
  0.8 0.6 broadcast_in_dim.17.dest_ref
  1.4 1.4 %broadcast_in_dim.18.gain_ref = f32[8,3584]{1,0:T(8,128)} broadcast(f32[3584]{0:T(1024)} %param.8), dimensions={1} | broadcast | bytes 129024 | tf_op jit(solution)/shard_map/broadcast_in_dim | solution.py:300
  2.8 85.9 %shard_map.55 = bf16[256,2560]{1,0:T(8,128)(2,1)} custom-call(s32[1,4]{1,0:T(1,128)} %lens_ref.1, s32[8,128]{1,0:T(8,128)} %broadcast_in_dim.17.dest_ref, bf16[128,3584]{1,0:T(8,128)(2,1)} %tok_ref.1, f32[8,3584]{1,0:T(8,128)} %broadcast_in_dim.18.gain_ref, bf16[448,2560]{1,0:T(8,128)(2,1)} %w_ref.1), custom_call_target="tpu_custom_call" | custom-call | tf_op jit(solution)/shard_map/pallas_call | solution.py:305
  88.7 2.5 %copy.7 = bf16[256,2560]{1,0:T(8,128)(2,1)} copy(bf16[256,2560]{1,0:T(8,128)(2,1)} %shard_map.55) | data formatting | bytes 2621440
